TPU v7x, 32 devices: a whole 2x2x4 slice. The times are simulated.
32 devices in a mesh: gx: 8 (over y, x, core), gy: 4 (over z).
Axes of the slice: x: 2, y: 2, z: 4, core: 2. Of those that a mesh axis runs over, the one named last changes fastest.
Arguments:
- nodes: bfloat16 [32768, 128], P(('gx', 'gy')), may hold values from -6 to 6
- ghost_rows: int32 [32, 8, 256], P(('gx', 'gy')), may hold values from 0 to 1023
- ghost_count: int32 [32, 8], P(('gx', 'gy')), may hold values from 0 to 256, as said below
- edge_send: int32 [32, 4096], P(('gx', 'gy')), may hold values from 0 to 3071
- edge_recv: int32 [32, 4096], P(('gx', 'gy')), may hold values from 0 to 1023
- edge_count: int32 [32], P(('gx', 'gy')), may hold values from 512 to 4096, as said below
- pool_map: int32 [32, 1024], P(('gx', 'gy')), may hold values from 0 to 191, as said below
- w_edge_in: bfloat16 [256, 128], replicated, may hold values from -0.375 to 0.375
- w_edge_out: bfloat16 [128, 128], replicated, may hold values from -0.5 to 0.5
- w_node_in: bfloat16 [256, 128], replicated, may hold values from -0.375 to 0.375
- w_node_out: bfloat16 [128, 128], replicated, may hold values from -0.5 to 0.5
- w_coarse_in: bfloat16 [128, 128], replicated, may hold values from -0.5 to 0.5
- w_coarse_out: bfloat16 [128, 128], replicated, may hold values from -0.5 to 0.5
- d_fine: bfloat16 [32768, 128], P(('gx', 'gy')), may hold values from -6 to 6
- d_coarse: bfloat16 [4096, 128], P(('gx', 'gy')), may hold values from -6 to 6
Outputs:
- fine_out: bfloat16 [32768, 128], P(('gx', 'gy'))
- coarse_out: bfloat16 [4096, 128], P(('gx', 'gy'))
- grad_nodes: float32 [32768, 128], P(('gx', 'gy'))
- grad_edge_in: float32 [256, 128], replicated
- grad_edge_out: float32 [128, 128], replicated
- grad_node_in: float32 [256, 128], replicated
- grad_node_out: float32 [128, 128], replicated
- grad_coarse_in: float32 [128, 128], replicated
- grad_coarse_out: float32 [128, 128], replicated
Inputs may be any that keep to these rules, and one draw needn't show every extreme that they name: `ghost_count`: every device fills all 256 slots for at least one offset. `edge_count`: at least one device has all 4096 slots live. `pool_map`: values under 32 occur only on devices that are not first along gy, and values of 160 or more only on devices that are not last along gy, so every parent lies in the device's gx column.
All inputs are finite; a program needn't handle non-finite values.
Results may differ from a plain program's by a relative error of at most 0.012.
Values may be sent and summed in bfloat16 or wider, within the bound.
A program may use at most 64 MiB of HBM per device.

v0:
```python
import jax
import jax.numpy as jnp
from jax import lax
from jax.sharding import PartitionSpec as P

BAND = 32


def with_halo(x, sides, width):
    for axis, dim in sides:
        devices, length = (lax.axis_size(axis), x.shape[dim])
        up = [(i, (i + 1) % devices) for i in range(devices - 1)]
        down = [(j, i) for i, j in up]
        last = lax.slice_in_dim(x, length - width, length, axis=dim)
        initial = lax.slice_in_dim(x, 0, width, axis=dim)
        before = lax.ppermute(last, axis, up)
        after = lax.ppermute(initial, axis, down)
        x = jnp.concatenate([before, x, after], axis=dim)
    return x


def matmul(left, right):
    return jnp.dot(left, right, preferred_element_type=jnp.float32)


def silu_slope(pre_value):
    sigmoid_v = jax.nn.sigmoid(pre_value)
    return sigmoid_v * (1.0 + pre_value * (1.0 - sigmoid_v))


def fine_forward(owned, ghosts, send_index, recv_index, edge_live, weights):
    w_edge_in, w_edge_out, w_node_in, w_node_out = weights
    latent = owned.shape[1]
    lookup = jnp.concatenate([owned, ghosts], axis=0)
    senders = lookup[send_index]
    receivers = owned[recv_index]
    edge_pre = matmul(senders, w_edge_in[:latent]) + matmul(receivers, w_edge_in[latent:])
    edge_act = jax.nn.silu(edge_pre).astype(jnp.bfloat16)
    message = (matmul(edge_act, w_edge_out) * edge_live[:, None]).astype(jnp.bfloat16)
    summed = jax.ops.segment_sum(
        message.astype(jnp.float32), recv_index, num_segments=owned.shape[0]
    ).astype(jnp.bfloat16)
    node_pre = matmul(owned, w_node_in[:latent]) + matmul(summed, w_node_in[latent:])
    node_act = jax.nn.silu(node_pre).astype(jnp.bfloat16)
    fine_out = (owned.astype(jnp.float32) + matmul(node_act, w_node_out)).astype(jnp.bfloat16)
    return (fine_out, (senders, receivers, edge_pre, edge_act, summed, node_pre, node_act))


def fine_backward(owned, send_index, recv_index, edge_live, weights, stashed, d_total, lookup_rows):
    w_edge_in, w_edge_out, w_node_in, w_node_out = weights
    senders, receivers, edge_pre, edge_act, summed, node_pre, node_act = stashed
    rows_here, latent = owned.shape
    d_out16 = d_total.astype(jnp.bfloat16)
    g_node_out = matmul(node_act.T, d_out16)
    d_node_pre = (matmul(d_out16, w_node_out.T) * silu_slope(node_pre)).astype(jnp.bfloat16)
    g_node_in = jnp.concatenate([matmul(owned.T, d_node_pre), matmul(summed.T, d_node_pre)], axis=0)
    d_owned = d_total + matmul(d_node_pre, w_node_in[:latent].T)
    d_summed = matmul(d_node_pre, w_node_in[latent:].T).astype(jnp.bfloat16)
    d_message = d_summed[recv_index] * edge_live[:, None].astype(d_summed.dtype)
    g_edge_out = matmul(edge_act.T, d_message)
    d_edge_pre = (matmul(d_message, w_edge_out.T) * silu_slope(edge_pre)).astype(jnp.bfloat16)
    g_edge_in = jnp.concatenate(
        [matmul(senders.T, d_edge_pre), matmul(receivers.T, d_edge_pre)], axis=0
    )
    d_senders = matmul(d_edge_pre, w_edge_in[:latent].T)
    d_receivers = matmul(d_edge_pre, w_edge_in[latent:].T)
    d_lookup = jax.ops.segment_sum(d_senders, send_index, num_segments=lookup_rows)
    d_owned = (
        d_owned
        + d_lookup[:rows_here]
        + jax.ops.segment_sum(d_receivers, recv_index, num_segments=rows_here)
    )
    return (d_owned, d_lookup[rows_here:], (g_edge_in, g_edge_out, g_node_in, g_node_out))


def across_x(blocks):
    return with_halo(blocks, (("gx", 0),), 1)


def across_y(blocks):
    return with_halo(blocks, (("gy", 0),), 1)


def spread_ghosts(outgoing):
    first = across_x(jnp.stack([outgoing[0:3], outgoing[5:8]]))
    came_plus = first[0]
    came_minus = first[3]
    lower_blocks = jnp.stack([outgoing[3], came_minus[0], came_plus[0]])
    upper_blocks = jnp.stack([outgoing[4], came_minus[2], came_plus[2]])
    second = across_y(jnp.stack([lower_blocks, upper_blocks]))
    from_low = second[0]
    from_high = second[3]
    return jnp.stack(
        [
            from_high[1],
            came_minus[1],
            from_low[1],
            from_high[0],
            from_low[0],
            from_high[2],
            came_plus[1],
            from_low[2],
        ]
    )


def return_ghosts(d_blocks):
    lower_blocks = jnp.stack([d_blocks[4], d_blocks[2], d_blocks[7]])
    upper_blocks = jnp.stack([d_blocks[3], d_blocks[0], d_blocks[5]])
    third = across_y(jnp.stack([lower_blocks, upper_blocks]))
    from_low = third[0]
    from_high = third[3]
    minus_blocks = jnp.stack([from_low[2], d_blocks[6], from_high[2]])
    plus_blocks = jnp.stack([from_low[1], d_blocks[1], from_high[1]])
    fourth = across_x(jnp.stack([minus_blocks, plus_blocks]))
    back_low = fourth[0]
    back_high = fourth[3]
    return jnp.stack(
        [
            back_low[0],
            back_low[1],
            back_low[2],
            from_low[0],
            from_high[0],
            back_high[0],
            back_high[1],
            back_high[2],
        ]
    )


def body(
    nodes,
    ghost_rows,
    ghost_count,
    edge_send,
    edge_recv,
    edge_count,
    pool_map,
    w_edge_in,
    w_edge_out,
    w_node_in,
    w_node_out,
    w_coarse_in,
    w_coarse_out,
    d_fine,
    d_coarse,
):
    rows_here, latent = nodes.shape
    ghost_lists = ghost_rows[0]
    peer_count, slot_count = ghost_lists.shape
    slot_live = jnp.arange(slot_count, dtype=jnp.int32)[None, :] < ghost_count[0][:, None]
    outgoing = jnp.where(slot_live[:, :, None], nodes[ghost_lists], jnp.zeros((), nodes.dtype))
    arrived = spread_ghosts(outgoing)
    send_index = edge_send[0]
    recv_index = edge_recv[0]
    edge_live = (jnp.arange(send_index.shape[0], dtype=jnp.int32) < edge_count[0]).astype(
        jnp.float32
    )
    weights = (w_edge_in, w_edge_out, w_node_in, w_node_out)
    fine_out, stashed = fine_forward(
        nodes,
        arrived.reshape(peer_count * slot_count, latent),
        send_index,
        recv_index,
        edge_live,
        weights,
    )
    groups = lax.axis_size("gy")
    coarse_rows = d_coarse.shape[0]
    fine_wide = fine_out.astype(jnp.float32)
    parents = pool_map[0]
    window = jax.ops.segment_sum(fine_wide, parents, num_segments=coarse_rows + 2 * BAND)
    rims = with_halo(
        jnp.stack([window[:BAND], window[coarse_rows + BAND :]]).astype(jnp.bfloat16),
        (("gy", 0),),
        1,
    ).astype(jnp.float32)
    pooled = (
        window[BAND : coarse_rows + BAND]
        .at[:BAND]
        .add(rims[0])
        .at[coarse_rows - BAND :]
        .add(rims[3])
    )
    coarse_in = (0.125 * pooled).astype(jnp.bfloat16)
    coarse_pre = matmul(coarse_in, w_coarse_in)
    coarse_act = jax.nn.silu(coarse_pre).astype(jnp.bfloat16)
    coarse_out = (coarse_in.astype(jnp.float32) + matmul(coarse_act, w_coarse_out)).astype(
        jnp.bfloat16
    )
    g_coarse_out = matmul(coarse_act.T, d_coarse)
    d_coarse_pre = (matmul(d_coarse, w_coarse_out.T) * silu_slope(coarse_pre)).astype(jnp.bfloat16)
    g_coarse_in = matmul(coarse_in.T, d_coarse_pre)
    d_coarse_in = (d_coarse.astype(jnp.float32) + matmul(d_coarse_pre, w_coarse_in.T)).astype(
        jnp.bfloat16
    )
    reach = with_halo(d_coarse_in, (("gy", 0),), BAND)
    parent_grad = reach[parents]
    d_total = d_fine.astype(jnp.float32) + 0.125 * parent_grad.astype(jnp.float32)
    d_owned, d_ghosts, partials = fine_backward(
        nodes,
        send_index,
        recv_index,
        edge_live,
        weights,
        stashed,
        d_total,
        rows_here + peer_count * slot_count,
    )
    returned = return_ghosts(d_ghosts.astype(jnp.bfloat16).reshape(peer_count, slot_count, latent))
    returned = jnp.where(slot_live[:, :, None], returned.astype(jnp.float32), 0.0)
    d_owned = d_owned + jax.ops.segment_sum(
        returned.reshape(peer_count * slot_count, latent),
        ghost_lists.reshape(peer_count * slot_count),
        num_segments=rows_here,
    )
    totals = lax.psum(
        (partials[0], partials[1], partials[2], partials[3], g_coarse_in, g_coarse_out),
        ("gx", "gy"),
    )
    grad_scale = 1.0 / (rows_here * lax.axis_size("gx") * groups) ** 0.5
    return (
        fine_out,
        coarse_out,
        d_owned,
        totals[0] * grad_scale,
        totals[1] * grad_scale,
        totals[2] * grad_scale,
        totals[3] * grad_scale,
        totals[4] * grad_scale,
        totals[5] * grad_scale,
    )


def solution(mesh):
    placed = (
        P(("gx", "gy"), None),
        P(("gx", "gy"), None, None),
        P(("gx", "gy"), None),
        P(("gx", "gy"), None),
        P(("gx", "gy"), None),
        P(("gx", "gy")),
        P(("gx", "gy"), None),
        P(),
        P(),
        P(),
        P(),
        P(),
        P(),
        P(("gx", "gy"), None),
        P(("gx", "gy"), None),
    )
    return jax.shard_map(
        body,
        mesh=mesh,
        in_specs=placed,
        out_specs=(
            P(("gx", "gy"), None),
            P(("gx", "gy"), None),
            P(("gx", "gy"), None),
            P(),
            P(),
            P(),
            P(),
            P(),
            P(),
        ),
        check_vma=False,
    )
```

profile of v0, /device:TPU:0, one launch (start us, length us, event | category | flops | bytes accessed | tf_op | source)
XLA Modules:
  0.0 367.6 jit_solution(4808389094989532764)
XLA Ops:
  8.7 6.6 %gather_fusion = bf16[2048,128]{1,0:T(8,128)(2,1)S(1)} fusion(bf16[1024,128]{1,0:T(8,128)(2,1)} %param.19, s32[2048]{0:T(1024)S(1)} %broadcast_clamp_fusion.2), kind=kCustom, calls=%fused_computation | custom fusion | bytes 1056768 | tf_op jit(solution)/shard_map/gather | solution.py:153
  15.7 1.3 collective-permute-start
  17.0 3.0 collective-permute-start.1
  20.9 1.0 fusion.58
  21.9 12.1 %gather_fusion.2 = bf16[4096,128]{1,0:T(8,128)(2,1)S(1)} fusion(bf16[1024,128]{1,0:T(8,128)(2,1)S(1)} %copy-done.1, s32[4096]{0:T(1024)S(1)} %get-tuple-element.65), kind=kCustom, calls=%fused_computation.2 | custom fusion | bytes 2113536 | tf_op jit(solution)/shard_map/gather | solution.py:36
  34.7 1.3 collective-permute-start.2
  36.0 5.6 %collective-permute-start.3 = (bf16[1,3,256,128]{3,2,1,0:T(8,128)(2,1)S(1)}, bf16[1,3,256,128]{3,2,1,0:T(8,128)(2,1)S(1)}, u32[]{:S(2)}, u32[]{:S(2)}) collective-permute-start(bf16[1,3,256,128]{3,2,1,0:T(8,128)(2,1)S(1)} %maximum_bitcast_fusion.1), channel_id=1, source_target_pairs={{0,1},{1,2},{2,3},{4,5},{5,6},{6,7},{8,9},{9,10},{10,11},{12,13},{... | collective-permute-start | bytes 589832 | tf_op jit(solution)/shard_map/ppermute | solution.py:16
  41.6 3.2 collective-permute-done.2
  44.8 1.8 collective-permute-done.3
  46.8 12.1 %gather_fusion.1 = bf16[4096,128]{1,0:T(8,128)(2,1)S(1)} fusion(bf16[3072,128]{1,0:T(8,128)(2,1)S(1)} %pad_maximum_fusion, s32[4096]{0:T(1024)S(1)} %get-tuple-element.66), kind=kCustom, calls=%fused_computation.1 | custom fusion | bytes 2113536 | tf_op jit(solution)/shard_map/gather | solution.py:35
  59.3 2.0 multiply_convert_fusion
  61.4 2.0 fusion.1
  63.3 22.8 %scatter_custom_fusion = f32[1024,128]{1,0:T(8,128)S(1)} fusion(s32[4096]{0:T(1024)S(1)} %bitcast.185, f32[4096,128]{1,0:T(8,128)} %fusion.1, f32[]{:T(128)} %constant.79.clone.1), kind=kCustom, calls=%fused_computation.53 | custom fusion | flops 524288 | bytes 524800 | tf_op jit(solution)/shard_map/scatter-add | solution.py:40
  86.4 1.2 fusion.4
  87.6 6.2 %scatter_custom_fusion.1 = f32[192,128]{1,0:T(8,128)S(1)} fusion(s32[1024]{0:T(1024)} %bitcast.194, bf16[1024,128]{1,0:T(8,128)(2,1)S(1)} %fusion.4, f32[]{:T(128)} %constant.79.clone.1), kind=kCustom, calls=%fused_computation.45 | custom fusion | flops 262144 | bytes 360960 | tf_op jit(solution)/shard_map/scatter-add | solution.py:173
  93.9 4.4 %collective-permute-start.4 = (bf16[1,32,128]{2,1,0:T(8,128)(2,1)S(1)}, bf16[1,32,128]{2,1,0:T(8,128)(2,1)S(1)}, u32[]{:S(2)}, u32[]{:S(2)}) collective-permute-start(bf16[1,32,128]{2,1,0:T(8,128)(2,1)S(1)} %get-tuple-element.59), channel_id=1, source_target_pairs={{0,1},{1,2},{2,3},{4,5},{5,6},{6,7},{8,9},{9,10},{10,11},{12,13},{... | collective-permute-start | bytes 24584 | tf_op jit(solution)/shard_map/ppermute | solution.py:16
  98.3 1.3 collective-permute-start.5
  101.3 2.6 collective-permute-done.5
  104.1 0.9 fusion.7
  106.0 1.5 fusion.6
  107.5 3.9 %collective-permute-start.6 = (bf16[32,128]{1,0:T(8,128)(2,1)S(1)}, bf16[32,128]{1,0:T(8,128)(2,1)S(1)}, u32[]{:S(2)}, u32[]{:S(2)}) collective-permute-start(bf16[32,128]{1,0:T(8,128)(2,1)S(1)} %get-tuple-element.61), channel_id=1, source_target_pairs={{0,1},{1,2},{2,3},{4,5},{5,6},{6,7},{8,9},{9,10},{10,11},{12,13},{... | collective-permute-start | bytes 24584 | tf_op jit(solution)/shard_map/ppermute | solution.py:16
  111.4 1.5 collective-permute-start.7
  113.8 3.2 collective-permute-done.7
  117.0 3.2 gather_fusion.3
  120.2 1.5 fusion.5
  121.7 0.9 fusion.25
  123.1 15.0 %gather_fusion.4 = bf16[4096,128]{1,0:T(8,128)(2,1)} fusion(bf16[1024,128]{1,0:T(8,128)(2,1)S(1)} %convolution_convert_fusion, s32[4096]{0:T(1024)S(1)} %get-tuple-element.65), kind=kCustom, calls=%fused_computation.4 | custom fusion | bytes 2113536 | tf_op jit(solution)/shard_map/gather | solution.py:59
  138.1 3.3 fusion.10
  141.4 2.4 fusion.2
  144.8 1.8 fusion.50
  146.6 1.8 fusion.53
  148.3 23.0 %scatter_custom_fusion.2 = f32[3072,128]{1,0:T(8,128)S(1)} fusion(s32[4096]{0:T(1024)} %bitcast.191, f32[4096,128]{1,0:T(8,128)} %fusion.53, f32[]{:T(128)} %constant.79.clone.1), kind=kCustom, calls=%fused_computation.39 | custom fusion | flops 524288 | bytes 1573376 | tf_op jit(solution)/shard_map/scatter-add | solution.py:67
  173.1 4.2 %collective-permute-start.8 = (bf16[1,3,256,128]{3,2,1,0:T(8,128)(2,1)}, bf16[1,3,256,128]{3,2,1,0:T(8,128)(2,1)}, u32[]{:S(2)}, u32[]{:S(2)}) collective-permute-start(bf16[1,3,256,128]{3,2,1,0:T(8,128)(2,1)} %maximum_bitcast_fusion.2), channel_id=1, source_target_pairs={{0,1},{1,2},{2,3},{4,5},{5,6},{6,7},{8,9},{9,10},{10,11},{12,13},{... | collective-permute-start | bytes 589832 | tf_op jit(solution)/shard_map/ppermute | solution.py:16
  178.0 1.3 collective-permute-start.9
  180.6 22.6 %scatter_fusion = f32[1024,128]{1,0:T(8,128)S(1)} fusion(f32[1024,128]{1,0:T(8,128)S(1)} %fusion.3, s32[4096]{0:T(1024)S(1)} %bitcast.186, f32[4096,128]{1,0:T(8,128)S(1)} %copy-done.2), kind=kCustom, calls=%fused_computation.8 | custom fusion | flops 524288 | bytes 6307840 | tf_op jit(solution)/shard_map/scatter-add | solution.py:71
  203.2 2.0 fusion.28
  205.2 0.9 slice_bitcast_fusion.7
  206.1 0.9 slice_bitcast_fusion.5
  207.0 1.3 collective-permute-start.10
  208.4 1.3 collective-permute-start.11
  209.7 126.5 %all-reduce.3.cloned.1.call-done = (f32[256,128]{1,0:T(8,128)}, f32[128,128]{1,0:T(8,128)}, f32[256,128]{1,0:T(8,128)}, f32[128,128]{1,0:T(8,128)}, f32[128,128]{1,0:T(8,128)}, /*index=5*/f32[128,128]{1,0:T(8,128)}) async-done(((f32[256,128]{1,0:T(8,128)}, f32[128,128]{1,0:T(8,128)}, f32[256,128]{1,0:T(8,128)}, f32[128,128]{1,0:T(8,128)}, f32[128,128]{1,0:T(8,128)}, /*index=5*/f32[128,128]{1,0:T(8,128)}), ...) | async-done | bytes 524304 | tf_op jit(solution)/shard_map/psum | solution.py:218
  336.1 1.6 broadcast_multiply_fusion.1
  337.7 1.5 broadcast_multiply_fusion.5
  339.2 1.5 broadcast_multiply_fusion.4
  340.7 1.5 broadcast_multiply_fusion.3
  342.1 1.6 broadcast_multiply_fusion
  343.7 1.5 broadcast_multiply_fusion.2
  347.0 12.9 %scatter_custom_fusion.4 = f32[1024,128]{1,0:T(8,128)S(1)} fusion(s32[2048]{0:T(1024)} %bitcast.193, bf16[2048,128]{1,0:T(8,128)(2,1)S(1)} %bitcast.184, f32[]{:T(128)} %constant.79.clone.1, pred[2048]{0:T(1024)(128)(4,1)S(1)} %copy-done.23), kind=kCustom, calls=%fused_computation.34 | custom fusion | flops 786432 | bytes 1051648 | tf_op jit(solution)/shard_map/scatter-add | solution.py:213
  (126 shorter events, 15.2 us)
Async XLA Ops:
  7.2 54.2 %copy-start = (bf16[128,128]{1,0:T(8,128)(2,1)S(1)}, bf16[128,128]{1,0:T(8,128)(2,1)}, u32[]{:S(2)}) copy-start(bf16[128,128]{1,0:T(8,128)(2,1)} %param.27) | copy-start | bytes 98308
  7.2 328.9 %all-reduce.3.cloned.1.call-start = ((), (), s32[]{:S(2)}) async-start(), calls=%async_computation | async-start | bytes 1048576 | tf_op jit(solution)/shard_map/psum | solution.py:218
  8.0 7.4 %copy-start.19 = (pred[8,256]{1,0:T(8,128)(4,1)}, pred[8,256]{1,0:T(8,128)(4,1)S(1)}, u32[]{:S(2)}) copy-start(pred[8,256]{1,0:T(8,128)(4,1)S(1)} %iota_compare_fusion.1) | copy-start | bytes 6148
  15.3 5.5 %copy-start.25 = (s32[1,1024]{1,0:T(1,128)S(1)}, s32[1,1024]{1,0:T(1,128)}, u32[]{:S(2)}) copy-start(s32[1,1024]{1,0:T(1,128)} %param.25) | copy-start | bytes 12292
  15.3 5.5 %copy-start.22 = (s32[1,4096]{1,0:T(1,128)S(1)}, s32[1,4096]{1,0:T(1,128)}, u32[]{:S(2)}) copy-start(s32[1,4096]{1,0:T(1,128)} %param.22) | copy-start | bytes 49156
  15.3 5.5 %copy-start.16 = (s32[1,4096]{1,0:T(1,128)S(1)}, s32[1,4096]{1,0:T(1,128)}, u32[]{:S(2)}) copy-start(s32[1,4096]{1,0:T(1,128)} %param.23) | copy-start | bytes 49156
  15.3 5.5 %copy-start.1 = (bf16[1024,128]{1,0:T(8,128)(2,1)S(1)}, bf16[1024,128]{1,0:T(8,128)(2,1)}, u32[]{:S(2)}) copy-start(bf16[1024,128]{1,0:T(8,128)(2,1)} %param.19) | copy-start | bytes 786436
  15.3 5.5 %copy-start.8 = (bf16[256,128]{1,0:T(8,128)(2,1)S(1)}, bf16[256,128]{1,0:T(8,128)(2,1)}, u32[]{:S(2)}) copy-start(bf16[256,128]{1,0:T(8,128)(2,1)} %param.28) | copy-start | bytes 196612
  15.7 18.9 %collective-permute-start = (bf16[1,3,256,128]{3,2,1,0:T(8,128)(2,1)S(1)}, bf16[1,3,256,128]{3,2,1,0:T(8,128)(2,1)S(1)}, u32[]{:S(2)}, u32[]{:S(2)}) collective-permute-start(bf16[1,3,256,128]{3,2,1,0:T(8,128)(2,1)S(1)} %get-tuple-element.49), channel_id=1, source_target_pairs={{4,0},{8,4},{12,8},{16,12},{20,16},{24,20},{28,24},{5,1},{9,5},{13... | collective-permute-start | bytes 589832 | tf_op jit(solution)/shard_map/ppermute | solution.py:17
  17.0 17.6 %collective-permute-start.1 = (bf16[1,3,256,128]{3,2,1,0:T(8,128)(2,1)S(1)}, bf16[1,3,256,128]{3,2,1,0:T(8,128)(2,1)S(1)}, u32[]{:S(2)}, u32[]{:S(2)}) collective-permute-start(bf16[1,3,256,128]{3,2,1,0:T(8,128)(2,1)S(1)} %get-tuple-element.50), channel_id=1, source_target_pairs={{0,4},{4,8},{8,12},{12,16},{16,20},{20,24},{24,28},{1,5},{5,9},{9,... | collective-permute-start | bytes 589832 | tf_op jit(solution)/shard_map/ppermute | solution.py:16
  34.7 10.1 %collective-permute-start.2 = (bf16[1,3,256,128]{3,2,1,0:T(8,128)(2,1)S(1)}, bf16[1,3,256,128]{3,2,1,0:T(8,128)(2,1)S(1)}, u32[]{:S(2)}, u32[]{:S(2)}) collective-permute-start(bf16[1,3,256,128]{3,2,1,0:T(8,128)(2,1)S(1)} %maximum_bitcast_fusion), channel_id=1, source_target_pairs={{1,0},{2,1},{3,2},{5,4},{6,5},{7,6},{9,8},{10,9},{11,10},{13,12},{... | collective-permute-start | bytes 589832 | tf_op jit(solution)/shard_map/ppermute | solution.py:17
  36.0 10.6 %collective-permute-start.3 = (bf16[1,3,256,128]{3,2,1,0:T(8,128)(2,1)S(1)}, bf16[1,3,256,128]{3,2,1,0:T(8,128)(2,1)S(1)}, u32[]{:S(2)}, u32[]{:S(2)}) collective-permute-start(bf16[1,3,256,128]{3,2,1,0:T(8,128)(2,1)S(1)} %maximum_bitcast_fusion.1), channel_id=1, source_target_pairs={{0,1},{1,2},{2,3},{4,5},{5,6},{6,7},{8,9},{9,10},{10,11},{12,13},{... | collective-permute-start | bytes 589832 | tf_op jit(solution)/shard_map/ppermute | solution.py:16
  46.8 12.2 %copy-start.13 = (bf16[256,128]{1,0:T(8,128)(2,1)S(1)}, bf16[256,128]{1,0:T(8,128)(2,1)}, u32[]{:S(2)}) copy-start(bf16[256,128]{1,0:T(8,128)(2,1)} %param.26) | copy-start | bytes 196612
  61.4 2.0 copy-start.4
  61.4 24.8 %copy-start.3 = (f32[1024,128]{1,0:T(8,128)S(1)}, f32[1024,128]{1,0:T(8,128)}, u32[]{:S(2)}) copy-start(f32[1024,128]{1,0:T(8,128)} %fusion.58) | copy-start | bytes 1572868
  86.1 14.1 %copy-start.20 = (pred[8,256]{1,0:T(8,128)(4,1)S(1)}, pred[8,256]{1,0:T(8,128)(4,1)}, u32[]{:S(2)}) copy-start(pred[8,256]{1,0:T(8,128)(4,1)} %copy-done.19) | copy-start | bytes 6148
  86.1 14.6 %copy-start.17 = (s32[1,8,256]{2,1,0:T(8,128)S(1)}, s32[1,8,256]{2,1,0:T(8,128)}, u32[]{:S(2)}) copy-start(s32[1,8,256]{2,1,0:T(8,128)} %param.20) | copy-start | bytes 24580
  86.4 1.2 copy-start.6
  86.4 17.6 %copy-start.15 = (bf16[128,128]{1,0:T(8,128)(2,1)S(1)}, bf16[128,128]{1,0:T(8,128)(2,1)}, u32[]{:S(2)}) copy-start(bf16[128,128]{1,0:T(8,128)(2,1)} %param.30) | copy-start | bytes 98308
  86.4 17.7 %copy-start.18 = (bf16[128,128]{1,0:T(8,128)(2,1)S(1)}, bf16[128,128]{1,0:T(8,128)(2,1)}, u32[]{:S(2)}) copy-start(bf16[128,128]{1,0:T(8,128)(2,1)} %param.33) | copy-start | bytes 98308
  86.4 30.6 %copy-start.21 = (s32[1024]{0:T(1024)S(1)}, s32[1024]{0:T(1024)}, u32[]{:S(2)}) copy-start(s32[1024]{0:T(1024)} %broadcast_clamp_fusion.3) | copy-start | bytes 12292
  87.6 29.4 %copy-start.10 = (bf16[1024,128]{1,0:T(8,128)(2,1)}, bf16[1024,128]{1,0:T(8,128)(2,1)S(1)}, u32[]{:S(2)}) copy-start(bf16[1024,128]{1,0:T(8,128)(2,1)S(1)} %fusion.4) | copy-start | bytes 786436
  93.9 7.5 %collective-permute-start.4 = (bf16[1,32,128]{2,1,0:T(8,128)(2,1)S(1)}, bf16[1,32,128]{2,1,0:T(8,128)(2,1)S(1)}, u32[]{:S(2)}, u32[]{:S(2)}) collective-permute-start(bf16[1,32,128]{2,1,0:T(8,128)(2,1)S(1)} %get-tuple-element.59), channel_id=1, source_target_pairs={{0,1},{1,2},{2,3},{4,5},{5,6},{6,7},{8,9},{9,10},{10,11},{12,13},{... | collective-permute-start | bytes 24584 | tf_op jit(solution)/shard_map/ppermute | solution.py:16
  98.3 5.7 %collective-permute-start.5 = (bf16[1,32,128]{2,1,0:T(8,128)(2,1)S(1)}, bf16[1,32,128]{2,1,0:T(8,128)(2,1)S(1)}, u32[]{:S(2)}, u32[]{:S(2)}) collective-permute-start(bf16[1,32,128]{2,1,0:T(8,128)(2,1)S(1)} %get-tuple-element.60), channel_id=1, source_target_pairs={{1,0},{2,1},{3,2},{5,4},{6,5},{7,6},{9,8},{10,9},{11,10},{13,12},{... | collective-permute-start | bytes 24584 | tf_op jit(solution)/shard_map/ppermute | solution.py:17
  107.5 6.2 %collective-permute-start.6 = (bf16[32,128]{1,0:T(8,128)(2,1)S(1)}, bf16[32,128]{1,0:T(8,128)(2,1)S(1)}, u32[]{:S(2)}, u32[]{:S(2)}) collective-permute-start(bf16[32,128]{1,0:T(8,128)(2,1)S(1)} %get-tuple-element.61), channel_id=1, source_target_pairs={{0,1},{1,2},{2,3},{4,5},{5,6},{6,7},{8,9},{9,10},{10,11},{12,13},{... | collective-permute-start | bytes 24584 | tf_op jit(solution)/shard_map/ppermute | solution.py:16
  111.4 5.5 %collective-permute-start.7 = (bf16[32,128]{1,0:T(8,128)(2,1)S(1)}, bf16[32,128]{1,0:T(8,128)(2,1)S(1)}, u32[]{:S(2)}, u32[]{:S(2)}) collective-permute-start(bf16[32,128]{1,0:T(8,128)(2,1)S(1)} %get-tuple-element.62), channel_id=1, source_target_pairs={{1,0},{2,1},{3,2},{5,4},{6,5},{7,6},{9,8},{10,9},{11,10},{13,12},{... | collective-permute-start | bytes 24584 | tf_op jit(solution)/shard_map/ppermute | solution.py:17
  123.1 15.0 %copy-start.24 = (bf16[4096]{0:T(1024)(128)(2,1)S(1)}, bf16[4096]{0:T(1024)(128)(2,1)}, u32[]{:S(2)}) copy-start(bf16[4096]{0:T(1024)(128)(2,1)} %fusion.65) | copy-start | bytes 24580
  138.1 3.3 copy-start.5
  143.8 1.0 copy-start.14
  146.6 24.8 %copy-start.9 = (bf16[1024,128]{1,0:T(8,128)(2,1)S(1)}, bf16[1024,128]{1,0:T(8,128)(2,1)}, u32[]{:S(2)}) copy-start(bf16[1024,128]{1,0:T(8,128)(2,1)} %param.32) | copy-start | bytes 786436
  171.6 7.7 %copy-start.12 = (f32[128,128]{1,0:T(8,128)S(1)}, f32[128,128]{1,0:T(8,128)}, u32[]{:S(2)}) copy-start(f32[128,128]{1,0:T(8,128)} %fusion.25) | copy-start | bytes 196612
  171.7 8.9 %copy-start.2 = (f32[4096,128]{1,0:T(8,128)S(1)}, f32[4096,128]{1,0:T(8,128)}, u32[]{:S(2)}) copy-start(f32[4096,128]{1,0:T(8,128)} %fusion.50) | copy-start | bytes 6291460
  173.1 32.1 %collective-permute-start.8 = (bf16[1,3,256,128]{3,2,1,0:T(8,128)(2,1)}, bf16[1,3,256,128]{3,2,1,0:T(8,128)(2,1)}, u32[]{:S(2)}, u32[]{:S(2)}) collective-permute-start(bf16[1,3,256,128]{3,2,1,0:T(8,128)(2,1)} %maximum_bitcast_fusion.2), channel_id=1, source_target_pairs={{0,1},{1,2},{2,3},{4,5},{5,6},{6,7},{8,9},{9,10},{10,11},{12,13},{... | collective-permute-start | bytes 589832 | tf_op jit(solution)/shard_map/ppermute | solution.py:16
  178.0 28.1 %collective-permute-start.9 = (bf16[1,3,256,128]{3,2,1,0:T(8,128)(2,1)}, bf16[1,3,256,128]{3,2,1,0:T(8,128)(2,1)}, u32[]{:S(2)}, u32[]{:S(2)}) collective-permute-start(bf16[1,3,256,128]{3,2,1,0:T(8,128)(2,1)} %maximum_bitcast_fusion.3), channel_id=1, source_target_pairs={{1,0},{2,1},{3,2},{5,4},{6,5},{7,6},{9,8},{10,9},{11,10},{13,12},{... | collective-permute-start | bytes 589832 | tf_op jit(solution)/shard_map/ppermute | solution.py:17
  180.6 22.6 %copy-start.7 = (f32[1024,128]{1,0:T(8,128)S(1)}, f32[1024,128]{1,0:T(8,128)}, u32[]{:S(2)}) copy-start(f32[1024,128]{1,0:T(8,128)} %copy-done.6) | copy-start | bytes 1572868
  203.2 3.8 %copy-start.11 = (bf16[1,256,128]{2,1,0:T(8,128)(2,1)S(1)}, bf16[1,256,128]{2,1,0:T(8,128)(2,1)}, u32[]{:S(2)}) copy-start(bf16[1,256,128]{2,1,0:T(8,128)(2,1)} %get-tuple-element.43) | copy-start | bytes 196612
  205.2 141.8 %copy-start.23 = (pred[2048]{0:T(1024)(128)(4,1)S(1)}, pred[2048]{0:T(1024)(128)(4,1)}, u32[]{:S(2)}) copy-start(pred[2048]{0:T(1024)(128)(4,1)} %lt.95) | copy-start | bytes 6148
  207.0 138.1 %collective-permute-start.10 = (bf16[1,3,256,128]{3,2,1,0:T(8,128)(2,1)S(1)}, bf16[1,3,256,128]{3,2,1,0:T(8,128)(2,1)S(1)}, u32[]{:S(2)}, u32[]{:S(2)}) collective-permute-start(bf16[1,3,256,128]{3,2,1,0:T(8,128)(2,1)S(1)} %maximum_bitcast_fusion.4), channel_id=1, source_target_pairs={{0,4},{4,8},{8,12},{12,16},{16,20},{20,24},{24,28},{1,5},{5,9},{9,... | collective-permute-start | bytes 589832 | tf_op jit(solution)/shard_map/ppermute | solution.py:16
  208.4 138.6 %collective-permute-start.11 = (bf16[1,3,256,128]{3,2,1,0:T(8,128)(2,1)S(1)}, bf16[1,3,256,128]{3,2,1,0:T(8,128)(2,1)S(1)}, u32[]{:S(2)}, u32[]{:S(2)}) collective-permute-start(bf16[1,3,256,128]{3,2,1,0:T(8,128)(2,1)S(1)} %maximum_bitcast_fusion.5), channel_id=1, source_target_pairs={{4,0},{8,4},{12,8},{16,12},{20,16},{24,20},{28,24},{5,1},{9,5},{13... | collective-permute-start | bytes 589832 | tf_op jit(solution)/shard_map/ppermute | solution.py:17
Sparse Core Ops, SparseCore 0:
  205.3 130.7 all-reduce.2
where the time goes:
time: 369 us; the launch traced here: 368 us
  waiting for transfers between devices  137 us (37%)
  other arithmetic  103 us (28%)
  local copies, waits for them, and re-layouts  54.7 us (15%)
  starting transfers between devices  30.4 us (8%)
  matrix products  26.4 us (7%)
  between operations  15.4 us (4%)
    psum x1, waiting for transfers between devices, body(): lax.psum((partials[0], partials[1], partials[2], partials[3], g_coarse_in...  126 us
    dot_general x24, matrix products, matmul(): return jnp.dot(left, right, preferred_element_type=jnp.float32)  26.4 us
    scatter-add x1, other arithmetic, fine_backward(): jax.ops.segment_sum(d_senders, send_index, num_segments=lookup_rows)  23 us
    scatter-add x1, other arithmetic, fine_forward(): jax.ops.segment_sum(message.astype(jnp.float32), recv_index, num_segments...  22.8 us
    scatter-add x1, other arithmetic, fine_backward(): jax.ops.segment_sum(d_receivers, recv_index, num_segments=rows_here)  22.6 us
    ppermute x6, starting transfers between devices, with_halo(): before = lax.ppermute(last, axis, up)  22.4 us
    gather x1, local copies, waits for them, and re-layouts, fine_backward(): d_message = d_summed[recv_index] * edge_live[:, None].astype(d_summed.dtype)  15 us
    scatter-add x1, other arithmetic, body(): jax.ops.segment_sum(returned.reshape(peer_count * slot_count, latent), gh...  12.9 us
  transfers between devices with their start and end apart: 13, of which 5 were waited for; matrix products, arithmetic and copies ran while one was open for 15% of the time, Pallas kernels for 0%

commit v1 on v0

v1 whole, which is shorter than its diff:
```python
import functools

import jax
import jax.numpy as jnp
from jax import lax
from jax.experimental import pallas as pl
from jax.experimental.pallas import tpu as pltpu
from jax.sharding import PartitionSpec as P

BAND = 32
MESH = pl.DeviceIdType.MESH
ACROSS = (-1, -1, -1, 0, 0, 1, 1, 1)
ALONG = (-1, 0, 1, -1, 1, -1, 0, 1)
F32 = jnp.float32
BF16 = jnp.bfloat16
FOLDS = 4


def mm(a, b):
    return jnp.dot(a, b, preferred_element_type=F32)


def mm_t(a, b):
    return lax.dot_general(a, b, (((1,), (1,)), ((), ())), preferred_element_type=F32)


def t_mm(a, b):
    return lax.dot_general(a, b, (((0,), (0,)), ((), ())), preferred_element_type=F32)


def sigmoid(v):
    return 1.0 / (1.0 + jnp.exp(-v))


def pick_lanes(col, width):
    ids = lax.broadcasted_iota(jnp.int32, (col.shape[0], width), 1)
    return jnp.where(ids == col, 1.0, 0.0).astype(BF16)


def pick_sublanes(row, start, height):
    ids = lax.broadcasted_iota(jnp.int32, (height, row.shape[1]), 0)
    return jnp.where(ids == row - start, 1.0, 0.0).astype(BF16)


def fold_of(index, height):
    hi = jnp.zeros_like(index)
    for j in range(1, FOLDS):
        hi = hi + jnp.where(index >= j * height, 1, 0)
    return hi


def gather_folded(col, table):
    height = table.shape[0]
    width = table.shape[1] // FOLDS
    hi = fold_of(col, height)
    wide = mm(pick_lanes(col - hi * height, height), table)
    out = wide[:, :width]
    for j in range(1, FOLDS):
        out = jnp.where(hi == j, wide[:, j * width : (j + 1) * width], out)
    return out


def spread_folds(values, hi):
    values = values.astype(F32)
    return jnp.concatenate(
        [jnp.where(hi == j, values, 0.0).astype(BF16) for j in range(FOLDS)], axis=1
    )


def scatter_folded(row, wide_ref, height, tile, write):
    width = wide_ref.shape[1] // FOLDS
    low = row - fold_of(row, height) * height
    for start in range(0, height, tile):
        sums = mm(pick_sublanes(low, start, tile), wide_ref[...])
        for j in range(FOLDS):
            write(j * height + start, sums[:, j * width : (j + 1) * width])


def write_folded(table, rows, latent):
    height = table.shape[0]
    for j in range(FOLDS):
        table[:, j * latent : (j + 1) * latent] = rows(j * height, height)


def outgoing_kernel(nodes_ref, col_ref, out_ref, table):
    latent = nodes_ref.shape[1]
    write_folded(table, lambda s, h: nodes_ref[s : s + h, :], latent)
    step = 512 if col_ref.shape[0] % 512 == 0 else col_ref.shape[0]
    for s in range(0, col_ref.shape[0], step):
        out_ref[s : s + step, :] = gather_folded(col_ref[s : s + step, :], table[...]).astype(BF16)


def forward_kernel(
    chunk, nodes_ref, ghosts_ref, send_ref, recv_ref, recv_row_ref, pool_row_ref,
    wei_ref, weo_ref, wni_ref, wno_ref,
    fine_ref, window_ref, pre_ref, node_pre_ref, summed_ref,
    lookup, send_table, recv_table, wide,
):
    rows, latent = nodes_ref.shape
    lookup[:rows, :] = nodes_ref[...]
    lookup[rows:, :] = ghosts_ref[...]
    write_folded(send_table, lambda s, h: mm(lookup[s : s + h, :], wei_ref[:latent, :]).astype(BF16), latent)
    write_folded(recv_table, lambda s, h: mm(nodes_ref[s : s + h, :], wei_ref[latent:, :]).astype(BF16), latent)

    def edges(i, carry):
        at = pl.ds(pl.multiple_of(i * chunk, chunk), chunk)
        recv = recv_ref[at, :]
        pre = gather_folded(send_ref[at, :], send_table[...]) + gather_folded(recv, recv_table[...])
        pre_ref[at, :] = pre
        act = (pre * sigmoid(pre)).astype(BF16)
        message = mm(act, weo_ref[...]).astype(BF16)
        wide[at, :] = spread_folds(message, fold_of(recv, rows // FOLDS))
        return carry

    lax.fori_loop(0, send_ref.shape[0] // chunk, edges, 0)

    def put(s, v):
        summed_ref[s : s + v.shape[0], :] = v.astype(BF16)

    scatter_folded(recv_row_ref[...], wide, rows // FOLDS, min(256, rows // FOLDS), put)
    node_pre = mm(nodes_ref[...], wni_ref[:latent, :]) + mm(summed_ref[...], wni_ref[latent:, :])
    node_pre_ref[...] = node_pre
    node_act = (node_pre * sigmoid(node_pre)).astype(BF16)
    fine = (nodes_ref[...].astype(F32) + mm(node_act, wno_ref[...])).astype(BF16)
    fine_ref[...] = fine
    window_ref[...] = mm(pick_sublanes(pool_row_ref[...], 0, window_ref.shape[0]), fine)


def halo_pair(n_gy, low, high, got, send_sem, recv_sem):
    b = lax.axis_index("gy")
    down = pltpu.make_async_remote_copy(
        src_ref=low, dst_ref=got.at[1], send_sem=send_sem.at[0], recv_sem=recv_sem.at[1],
        device_id=(lax.axis_index("gx"), jnp.maximum(b - 1, 0)), device_id_type=MESH)
    up = pltpu.make_async_remote_copy(
        src_ref=high, dst_ref=got.at[0], send_sem=send_sem.at[1], recv_sem=recv_sem.at[0],
        device_id=(lax.axis_index("gx"), jnp.minimum(b + 1, n_gy - 1)), device_id_type=MESH)

    @pl.when(b > 0)
    def _():
        down.start()

    @pl.when(b < n_gy - 1)
    def _():
        up.start()

    @pl.when(b == 0)
    def _():
        got[0] = jnp.zeros(got.shape[1:], got.dtype)

    @pl.when(b == n_gy - 1)
    def _():
        got[1] = jnp.zeros(got.shape[1:], got.dtype)

    @pl.when(b > 0)
    def _():
        down.wait_send()
        up.wait_recv()

    @pl.when(b < n_gy - 1)
    def _():
        up.wait_send()
        down.wait_recv()


def coarse_kernel(
    n_gy, window_ref, d_coarse_ref, wci_ref, wco_ref,
    out_ref, reach_ref, g_in_ref, g_out_ref,
    rims, got_rims, bands, got_bands, send_sem, recv_sem,
):
    co = d_coarse_ref.shape[0]
    a, b = lax.axis_index("gx"), lax.axis_index("gy")
    barrier = pltpu.get_barrier_semaphore()

    @pl.when(b > 0)
    def _():
        pl.semaphore_signal(barrier, inc=1, device_id=(a, jnp.maximum(b - 1, 0)), device_id_type=MESH)

    @pl.when(b < n_gy - 1)
    def _():
        pl.semaphore_signal(barrier, inc=1, device_id=(a, jnp.minimum(b + 1, n_gy - 1)), device_id_type=MESH)

    rims[0] = window_ref[:BAND, :].astype(BF16)
    rims[1] = window_ref[co + BAND :, :].astype(BF16)

    pl.semaphore_wait(barrier, jnp.where(b > 0, 1, 0) + jnp.where(b < n_gy - 1, 1, 0))
    halo_pair(n_gy, rims.at[0], rims.at[1], got_rims, send_sem.at[0], recv_sem.at[0])
    own = window_ref[BAND : co + BAND, :]
    pooled = jnp.concatenate(
        [
            own[:BAND] + got_rims[0].astype(F32),
            own[BAND : co - BAND],
            own[co - BAND :] + got_rims[1].astype(F32),
        ],
        axis=0,
    )
    coarse_in = (0.125 * pooled).astype(BF16)
    d_coarse = d_coarse_ref[...]
    pre = mm(coarse_in, wci_ref[...])
    s = sigmoid(pre)
    d_pre = (mm_t(d_coarse, wco_ref[...]) * (s * (1.0 + pre * (1.0 - s)))).astype(BF16)
    d_in = (d_coarse.astype(F32) + mm_t(d_pre, wci_ref[...])).astype(BF16)
    bands[0] = d_in[:BAND]
    bands[1] = d_in[co - BAND :]
    reach_ref[BAND : co + BAND, :] = d_in
    halo_pair(n_gy, bands.at[0], bands.at[1], got_bands, send_sem.at[1], recv_sem.at[1])
    act = (pre * s).astype(BF16)
    out_ref[...] = (coarse_in.astype(F32) + mm(act, wco_ref[...])).astype(BF16)
    g_out_ref[...] = t_mm(act, d_coarse)
    g_in_ref[...] = t_mm(coarse_in, d_pre)
    reach_ref[:BAND, :] = got_bands[0]
    reach_ref[co + BAND :, :] = got_bands[1]


def backward_kernel(
    chunk, nodes_ref, ghosts_ref, recv_ref, recv_row_ref, send_ref, send_row_ref, pool_ref,
    wei_ref, weo_ref, wni_ref, wno_ref,
    pre_ref, node_pre_ref, summed_ref, reach_ref, d_fine_ref, g_ci_ref, g_co_ref,
    d_owned_ref, d_ghost_ref, g_ref,
    table, recv_wide, send_wide, sums_s, sums_r, g_out,
):
    rows, latent = nodes_ref.shape
    total_rows = rows + ghosts_ref.shape[0]
    nodes = nodes_ref[...]
    d_total = d_fine_ref[...].astype(F32) + 0.125 * mm(
        pick_lanes(pool_ref[...], reach_ref.shape[0]), reach_ref[...]
    )
    d16 = d_total.astype(BF16)
    node_pre = node_pre_ref[...]
    s = sigmoid(node_pre)
    node_act = (node_pre * s).astype(BF16)
    d_node = (mm_t(d16, wno_ref[...]) * (s * (1.0 + node_pre * (1.0 - s)))).astype(BF16)
    base = 2 * latent
    g_ref[base + latent : base + 2 * latent, :] = t_mm(nodes, d_node)
    g_ref[base + 2 * latent : base + 3 * latent, :] = t_mm(summed_ref[...], d_node)
    g_ref[base + 3 * latent : base + 4 * latent, :] = t_mm(node_act, d16)
    g_ref[base + 4 * latent : base + 5 * latent, :] = g_ci_ref[...]
    g_ref[base + 5 * latent : base + 6 * latent, :] = g_co_ref[...]
    d_owned_ref[...] = d_total + mm_t(d_node, wni_ref[:latent, :])
    d_summed = mm_t(d_node, wni_ref[latent:, :]).astype(BF16)
    height = rows // FOLDS
    for j in range(FOLDS):
        table[:, j * latent : (j + 1) * latent] = d_summed[j * height : (j + 1) * height]
    g_out[...] = jnp.zeros_like(g_out)

    def edges(i, carry):
        at = pl.ds(pl.multiple_of(i * chunk, chunk), chunk)
        recv = recv_ref[at, :]
        d_message = gather_folded(recv, table[...]).astype(BF16)
        pre = pre_ref[at, :]
        sig = sigmoid(pre)
        act = (pre * sig).astype(BF16)
        g_out[...] += t_mm(act, d_message)
        d_pre = (mm_t(d_message, weo_ref[...]) * (sig * (1.0 + pre * (1.0 - sig)))).astype(BF16)
        recv_wide[at, :] = spread_folds(d_pre, fold_of(recv, height))
        send_wide[at, :] = spread_folds(d_pre, fold_of(send_ref[at, :], total_rows // FOLDS))
        return carry

    lax.fori_loop(0, send_ref.shape[0] // chunk, edges, 0)
    g_ref[base : base + latent, :] = g_out[...]

    def put_s(at, v):
        sums_s[at : at + v.shape[0], :] = v.astype(BF16)

    def put_r(at, v):
        sums_r[at : at + v.shape[0], :] = v.astype(BF16)

    scatter_folded(recv_row_ref[...], recv_wide, height, min(256, height), put_r)
    scatter_folded(send_row_ref[...], send_wide, total_rows // FOLDS, min(256, total_rows // FOLDS), put_s)
    w_send, w_recv = wei_ref[:latent, :], wei_ref[latent:, :]
    d_owned_ref[...] += mm_t(sums_s[:rows, :], w_send) + mm_t(sums_r[...], w_recv)
    d_ghost_ref[...] = mm_t(sums_s[rows:, :], w_send).astype(BF16)
    g_ref[:latent, :] = t_mm(nodes, sums_s[:rows, :]) + t_mm(ghosts_ref[...], sums_s[rows:, :])
    g_ref[latent:base, :] = t_mm(nodes, sums_r[...])


def neighbours(n_gx, n_gy, sign):
    a, b = lax.axis_index("gx"), lax.axis_index("gy")
    found = []
    for dx, dy in zip(ACROSS, ALONG):
        dx, dy = sign * dx, sign * dy
        ta, tb = a + dx, b + dy
        sa, sb = a - dx, b - dy
        there = (ta >= 0) & (ta < n_gx) & (tb >= 0) & (tb < n_gy)
        here = (sa >= 0) & (sa < n_gx) & (sb >= 0) & (sb < n_gy)
        target = (jnp.clip(ta, 0, n_gx - 1), jnp.clip(tb, 0, n_gy - 1))
        found.append((target, there, here))
    return found


def greet(barrier, found):
    for target, there, _ in found:
        @pl.when(there)
        def _(target=target):
            pl.semaphore_signal(barrier, inc=1, device_id=target, device_id_type=MESH)


def greeted(barrier, found, more=0):
    count = jnp.int32(more)
    for _, there, _ in found:
        count = count + jnp.where(there, 1, 0)
    pl.semaphore_wait(barrier, count)


def exchange_copies(found, src_ref, dst_ref, send_sem, recv_sem):
    return [
        pltpu.make_async_remote_copy(
            src_ref=src_ref.at[k], dst_ref=dst_ref.at[k], send_sem=send_sem.at[k],
            recv_sem=recv_sem.at[k], device_id=found[k][0], device_id_type=MESH)
        for k in range(len(found))
    ]


def exchange_start(found, copies, dst_ref):
    for k in range(len(found)):
        @pl.when(found[k][1])
        def _(k=k):
            copies[k].start()

    for k in range(len(found)):
        @pl.when(jnp.logical_not(found[k][2]))
        def _(k=k):
            dst_ref[k] = jnp.zeros(dst_ref.shape[1:], dst_ref.dtype)


def exchange_wait(found, copies):
    for k in range(len(found)):
        @pl.when(found[k][1])
        def _(k=k):
            copies[k].wait_send()

        @pl.when(found[k][2])
        def _(k=k):
            copies[k].wait_recv()


def exchange_kernel(n_gx, n_gy, src_ref, dst_ref, send_sem, recv_sem):
    found = neighbours(n_gx, n_gy, 1)
    barrier = pltpu.get_barrier_semaphore()
    greet(barrier, found)
    greeted(barrier, found)
    copies = exchange_copies(found, src_ref, dst_ref, send_sem, recv_sem)
    exchange_start(found, copies, dst_ref)
    exchange_wait(found, copies)


def reduce_kernel(
    n_gx, n_gy, ghost_ref, g_ref, back_ref, total_ref,
    g16, got_x, mid, got_y, ghost_send, ghost_recv, xs, xr, ys, yr, xs2, xr2, ys2, yr2,
):
    a, b = lax.axis_index("gx"), lax.axis_index("gy")
    found = neighbours(n_gx, n_gy, -1)
    peers_x = [(lax.rem(a + r, n_gx), b) for r in range(1, n_gx)]
    peers_y = [(a, lax.rem(b + r, n_gy)) for r in range(1, n_gy)]
    barrier = pltpu.get_barrier_semaphore()
    corners = [f for f, dx, dy in zip(found, ACROSS, ALONG) if dx and dy]
    greet(barrier, corners)
    for peer in peers_x + peers_y:
        pl.semaphore_signal(barrier, inc=1, device_id=peer, device_id_type=MESH)
    g16[...] = g_ref[...].astype(BF16)
    greeted(barrier, corners, n_gx + n_gy - 2)

    def remote(src, dst, send, recv, peer):
        return pltpu.make_async_remote_copy(
            src_ref=src, dst_ref=dst, send_sem=send, recv_sem=recv, device_id=peer, device_id_type=MESH)

    first = [
        remote(g16.at[p[0]], got_x.at[r], xs.at[r], xr.at[r], p) for r, p in enumerate(peers_x)
    ]
    for copy in first:
        copy.start()
    copies = exchange_copies(found, ghost_ref, back_ref, ghost_send, ghost_recv)
    exchange_start(found, copies, back_ref)
    total = g_ref[a]
    for r, copy in enumerate(first):
        copy.wait_recv()
        total = total + got_x[r].astype(F32)
    mid[...] = total.astype(BF16)
    second = [
        remote(mid.at[p[1]], got_y.at[r], ys.at[r], yr.at[r], p) for r, p in enumerate(peers_y)
    ]
    for copy in second:
        copy.start()
    final = mid[b].astype(F32)
    for r, copy in enumerate(second):
        copy.wait_recv()
        final = final + got_y[r].astype(F32)
    total_ref[a, b] = final.astype(BF16)
    third = [
        remote(total_ref.at[a, b], total_ref.at[a, b], ys2.at[r], yr2.at[r], p) for r, p in enumerate(peers_y)
    ]
    for copy in third:
        copy.start()
    for copy in third:
        copy.wait_recv()
    fourth = [
        remote(total_ref.at[a], total_ref.at[a], xs2.at[r], xr2.at[r], p) for r, p in enumerate(peers_x)
    ]
    for copy in fourth:
        copy.start()
    for copy in fourth:
        copy.wait_recv()
    exchange_wait(found, copies)
    for copy in first + second + third + fourth:
        copy.wait_send()


def final_kernel(
    scale, d_owned_ref, back_ref, col_ref, row_ref, total_ref,
    nodes_out, ei_ref, eo_ref, ni_ref, no_ref, ci_ref, co_ref, wide,
):
    height = d_owned_ref.shape[0] // FOLDS
    wide[...] = spread_folds(back_ref[...], fold_of(col_ref[...], height))

    def put(at, v):
        nodes_out[at : at + v.shape[0], :] = d_owned_ref[at : at + v.shape[0], :] + v

    scatter_folded(row_ref[...], wide, height, min(256, height), put)
    at = 0
    for ref in (ei_ref, eo_ref, ni_ref, no_ref, ci_ref, co_ref):
        ref[...] = total_ref[at : at + ref.shape[0], :].astype(F32) * scale
        at += ref.shape[0]


def call(kernel, outs, scratch, args, collective_id=None):
    extra = {}
    if collective_id is not None:
        extra = dict(collective_id=collective_id, has_side_effects=True)
    vmem = pl.BlockSpec(memory_space=pltpu.VMEM)
    return pl.pallas_call(
        kernel,
        out_shape=[jax.ShapeDtypeStruct(shape, kind) for shape, kind in outs],
        in_specs=[vmem] * len(args),
        out_specs=[vmem] * len(outs),
        scratch_shapes=scratch,
        compiler_params=pltpu.CompilerParams(vmem_limit_bytes=56 * 1024 * 1024, **extra),
    )(*args)


def body(
    n_gx, n_gy, nodes, ghost_rows, ghost_count, edge_send, edge_recv, edge_count, pool_map,
    w_edge_in, w_edge_out, w_node_in, w_node_out, w_coarse_in, w_coarse_out, d_fine, d_coarse,
):
    rows, latent = nodes.shape
    _, peers, slots = ghost_rows.shape
    ghosts_n = peers * slots
    edges_n = edge_send.shape[1]
    co = d_coarse.shape[0]
    chunk = 512 if edges_n % 512 == 0 else edges_n
    dma = pltpu.SemaphoreType.DMA
    live = jnp.arange(slots, dtype=jnp.int32)[None, :] < ghost_count[0][:, None]
    ghost_index = jnp.where(live, ghost_rows[0], -1).reshape(1, ghosts_n)
    ghost_col = ghost_index.reshape(ghosts_n, 1)
    edge_live = jnp.arange(edges_n, dtype=jnp.int32) < edge_count[0]
    recv_row = jnp.where(edge_live, edge_recv[0], -1).reshape(1, edges_n)
    recv_col = recv_row.reshape(edges_n, 1)
    send_row = edge_send
    send_col = edge_send.reshape(edges_n, 1)
    pool_col = pool_map.reshape(rows, 1)
    fold_rows = rows // FOLDS
    fold_all = (rows + ghosts_n) // FOLDS

    (outgoing,) = call(
        outgoing_kernel, [((ghosts_n, latent), BF16)],
        [pltpu.VMEM((fold_rows, FOLDS * latent), BF16)], (nodes, ghost_col))
    (arrived,) = call(
        functools.partial(exchange_kernel, n_gx, n_gy), [((peers, slots, latent), BF16)],
        [dma((peers,)), dma((peers,))], (outgoing.reshape(peers, slots, latent),), 0)
    ghosts = arrived.reshape(ghosts_n, latent)
    fine_out, window, pre, node_pre, summed = call(
        functools.partial(forward_kernel, chunk),
        [((rows, latent), BF16), ((co + 2 * BAND, latent), F32), ((edges_n, latent), F32),
         ((rows, latent), F32), ((rows, latent), BF16)],
        [pltpu.VMEM((rows + ghosts_n, latent), BF16), pltpu.VMEM((fold_all, FOLDS * latent), BF16),
         pltpu.VMEM((fold_rows, FOLDS * latent), BF16), pltpu.VMEM((edges_n, FOLDS * latent), BF16)],
        (nodes, ghosts, send_col, recv_col, recv_row, pool_map, w_edge_in, w_edge_out, w_node_in, w_node_out))
    coarse_out, reach, g_ci, g_co = call(
        functools.partial(coarse_kernel, n_gy),
        [((co, latent), BF16), ((co + 2 * BAND, latent), BF16), ((latent, latent), F32), ((latent, latent), F32)],
        [pltpu.VMEM((2, BAND, latent), BF16)] * 4 + [dma((2, 2)), dma((2, 2))],
        (window, d_coarse, w_coarse_in, w_coarse_out), 1)
    d_owned, d_ghosts, partial = call(
        functools.partial(backward_kernel, chunk),
        [((rows, latent), F32), ((ghosts_n, latent), BF16), ((8 * latent, latent), F32)],
        [pltpu.VMEM((fold_rows, FOLDS * latent), BF16), pltpu.VMEM((edges_n, FOLDS * latent), BF16),
         pltpu.VMEM((edges_n, FOLDS * latent), BF16), pltpu.VMEM((rows + ghosts_n, latent), BF16),
         pltpu.VMEM((rows, latent), BF16), pltpu.VMEM((latent, latent), F32)],
        (nodes, ghosts, recv_col, recv_row, send_col, send_row, pool_col, w_edge_in, w_edge_out, w_node_in,
         w_node_out, pre, node_pre, summed, reach, d_fine, g_ci, g_co))
    share = 8 * latent // (n_gx * n_gy)
    parts = (n_gx, n_gy, share, latent)
    back, total = call(
        functools.partial(reduce_kernel, n_gx, n_gy),
        [((peers, slots, latent), BF16), (parts, BF16)],
        [pltpu.VMEM(parts, BF16), pltpu.VMEM((n_gx - 1,) + parts[1:], BF16), pltpu.VMEM(parts[1:], BF16),
         pltpu.VMEM((n_gy - 1,) + parts[2:], BF16), dma((peers,)), dma((peers,))]
        + [dma((n_gx - 1,))] * 2 + [dma((n_gy - 1,))] * 2 + [dma((n_gx - 1,))] * 2 + [dma((n_gy - 1,))] * 2,
        (d_ghosts.reshape(peers, slots, latent), partial.reshape(parts)), 2)
    scale = 1.0 / (rows * n_gx * n_gy) ** 0.5
    outs = call(
        functools.partial(final_kernel, scale),
        [((rows, latent), F32), ((2 * latent, latent), F32), ((latent, latent), F32), ((2 * latent, latent), F32),
         ((latent, latent), F32), ((latent, latent), F32), ((latent, latent), F32)],
        [pltpu.VMEM((ghosts_n, FOLDS * latent), BF16)],
        (d_owned, back.reshape(ghosts_n, latent), ghost_col, ghost_index, total.reshape(8 * latent, latent)))
    return (fine_out, coarse_out) + tuple(outs)


def solution(mesh):
    split = P(("gx", "gy"), None)
    return jax.shard_map(
        functools.partial(body, mesh.shape["gx"], mesh.shape["gy"]),
        mesh=mesh,
        in_specs=(split, P(("gx", "gy"), None, None), split, split, split, P(("gx", "gy")), split)
        + (P(),) * 6
        + (split, split),
        out_specs=(split, split, split) + (P(),) * 6,
        check_vma=False,
    )
```

time: 369 us -> 97.9 us (0.27)
  waiting for transfers between devices: 137 us -> 0 us
  other arithmetic: 103 us -> 5.3 us
  Pallas kernels: 0 us -> 84.2 us
  local copies, waits for them, and re-layouts: 54.7 us -> 6.58 us
  starting transfers between devices: 30.4 us -> 0 us
  matrix products: 26.4 us -> 0 us
  between operations: 15.4 us -> 1.37 us
    psum x1 -> x0, waiting for transfers between devices: 126 us -> none  [body(): lax.psum((partials[0], partials[1], partials[2], partials[3], g_coarse_in...]
    scatter-add x7 -> x0, other arithmetic: 87.5 us -> none  [the longest x1 23 us: fine_backward(): jax.ops.segment_sum(d_senders, send_index, num_segments=lookup_rows)]
    pallas_call x0 -> x7, Pallas kernels: none -> 84.2 us  [call(): pl.pallas_call(kernel, out_shape=[jax.ShapeDtypeStruct(shape, kind) for s...]
    gather x5 -> x0, local copies, waits for them, and re-layouts: 49 us -> none  [the longest x1 15 us: fine_backward(): d_message = d_summed[recv_index] * edge_live[:, None].astype(d_summed.dtype)]
    ppermute x12 -> x0, starting transfers between devices: 30.3 us -> none  [the longest x6 22.4 us: with_halo(): before = lax.ppermute(last, axis, up)]
    dot_general x24 -> x0, matrix products: 26.4 us -> none  [matmul(): return jnp.dot(left, right, preferred_element_type=jnp.float32)]
    ppermute x12 -> x0, waiting for transfers between devices: 10.8 us -> none  [the longest x6 9.02 us: with_halo(): after = lax.ppermute(initial, axis, down)]
    mul x6 -> x0, other arithmetic: 9.04 us -> none  [the longest x1 1.57 us: body(): totals[0] * grad_scale]
  transfers between devices with their start and end apart: 13 -> 0, of which waited for: 5 -> 0; matrix products, arithmetic and copies ran while one was open for 15% -> 0% of each run, Pallas kernels for 0% -> 0%
where the time goes in v1:
time: 97.9 us; the launch traced here: 97.5 us
  Pallas kernels  84.2 us (86%)
  local copies, waits for them, and re-layouts  6.58 us (7%)
  other arithmetic  5.3 us (5%)
  between operations  1.37 us (1%)
    pallas_call x7, Pallas kernels, call(): pl.pallas_call(kernel, out_shape=[jax.ShapeDtypeStruct(shape, kind) for s...  84.2 us
    select_n x2, other arithmetic, body(): recv_row = jnp.where(edge_live, edge_recv[0], -1).reshape(1, edges_n)  2.86 us
    unnamed x11, local copies, waits for them, and re-layouts  2.19 us
    reshape x1, local copies, waits for them, and re-layouts, body(): send_col = edge_send.reshape(edges_n, 1)  2 us

profile of v1, /device:TPU:0, one launch (start us, length us, event | category | flops | bytes accessed | tf_op | source)
XLA Modules:
  0.0 97.5 jit_solution(17158532373976939193)
XLA Ops:
  1.3 0.7 fusion.1
  2.0 0.7 copy.32
  2.7 0.6 broadcast_select_fusion.row_ref
  3.4 1.3 %compare_select_fusion.recv_row_ref = s32[1,4096]{1,0:T(1,128)} fusion(s32[1,4096]{1,0:T(1,128)} %param.19, s32[]{:T(128)} %bitcast.27), kind=kLoop, calls=%fused_computation.3 | loop fusion | flops 8192 | bytes 32772 | tf_op jit(solution)/shard_map/jit(_where)/select_n | solution.py:454
  4.7 0.5 copy.31
  5.2 1.8 %copy.29.pool_ref = s32[1024,1]{1,0:T(8,128)} copy(s32[1024,1]{0,1:T(1,128)} %bitcast.41) | data formatting | bytes 8192 | tf_op jit(solution)/shard_map/reshape | solution.py:458
  6.9 0.4 copy.33
  7.3 0.0 copy-start
  7.3 1.1 %bitcast_select_fusion.col_ref = s32[2048,1]{1,0:T(8,128)} fusion(s32[1,2048]{0,1:T(8,128)S(1)} %copy.33, pred[1,2048]{0,1:T(8,128)(4,1)S(1)} %copy.31), kind=kLoop, calls=%fused_computation.2 | loop fusion | flops 2048 | bytes 18432 | tf_op jit(solution)/shard_map/jit(_where)/select_n | solution.py:451
  8.4 0.0 copy-start.1
  8.4 3.5 %shard_map.214 = bf16[2048,128]{1,0:T(8,128)(2,1)} custom-call(bf16[1024,128]{1,0:T(8,128)(2,1)} %nodes_ref.5, s32[2048,1]{1,0:T(8,128)} %bitcast_select_fusion.col_ref), custom_call_target="tpu_custom_call" | custom-call | tf_op jit(solution)/shard_map/pallas_call | solution.py:429
  11.9 9.9 %shard_map.215 = bf16[8,256,128]{2,1,0:T(8,128)(2,1)} custom-call(bf16[8,256,128]{2,1,0:T(8,128)(2,1)} %bitcast.30), custom_call_target="tpu_custom_call" | custom-call | tf_op jit(solution)/shard_map/pallas_call | solution.py:429
  21.8 0.0 copy-done
  21.8 2.0 %copy.27.send_ref = s32[4096,1]{1,0:T(8,128)} copy(s32[4096,1]{0,1:T(1,128)S(1)} %bitcast.39) | data formatting | bytes 32768 | tf_op jit(solution)/shard_map/reshape | solution.py:457
  23.8 0.0 copy-done.1
  23.8 0.6 copy.26
  24.5 1.5 %fusion.recv_ref = s32[4096,1]{1,0:T(8,128)} fusion(s32[4096,1]{1,0:T(8,128)S(1)} %copy.26, s32[]{:T(128)} %bitcast.26), kind=kLoop, calls=%fused_computation.1 | loop fusion | flops 8192 | bytes 32772 | tf_op jit(solution)/shard_map/jit(_where)/select_n | solution.py:454
  26.0 14.5 %shard_map.216 = (bf16[1024,128]{1,0:T(8,128)(2,1)}, f32[192,128]{1,0:T(8,128)}, f32[4096,128]{1,0:T(8,128)}, f32[1024,128]{1,0:T(8,128)}, bf16[1024,128]{1,0:T(8,128)(2,1)}) custom-call(bf16[1024,128]{1,0:T(8,128)(2,1)} %nodes_ref.5, bf16[2048,128]{1,0:T(8,128)(2,1)} %bitcast.28, s32[4096,1]{1,0:T(8,128)} %copy.27.send_ref, s32[4096,1]{1,0:T(8,128)} %fusion.recv_ref, ...), custom_call_target="tpu_custom_call" | custom-call | tf_op jit(solution)/shard_map/pallas_call | solution.py:429
  40.5 9.0 %shard_map.217 = (bf16[128,128]{1,0:T(8,128)(2,1)}, bf16[192,128]{1,0:T(8,128)(2,1)}, f32[128,128]{1,0:T(8,128)}, f32[128,128]{1,0:T(8,128)}) custom-call(f32[192,128]{1,0:T(8,128)} %get-tuple-element.31.window_ref, bf16[128,128]{1,0:T(8,128)(2,1)} %d_coarse_ref.1, bf16[128,128]{1,0:T(8,128)(2,1)} %wci_ref.1, bf16[128,128]{1,0:T(8,128)(2,1)} %wco_ref.1), custom_call_target="tpu_custom_call" | custom-call | tf_op jit(solution)/shard_map/pallas_call | solution.py:429
  49.5 17.7 %shard_map.218 = (f32[1024,128]{1,0:T(8,128)}, bf16[2048,128]{1,0:T(8,128)(2,1)}, f32[1024,128]{1,0:T(8,128)}) custom-call(bf16[1024,128]{1,0:T(8,128)(2,1)} %nodes_ref.5, bf16[2048,128]{1,0:T(8,128)(2,1)} %bitcast.29, s32[4096,1]{1,0:T(8,128)} %fusion.recv_ref, s32[1,4096]{1,0:T(1,128)} %compare_select_fusion.recv_row_ref, s32[4096,1]{1,0:T(8,128)} %copy.27.send_ref, ...), custom_call_target="tpu_custom_call" | custom-call | tf_op jit(solution)/shard_map/pallas_call | solution.py:429
  67.2 0.0 copy-start.2
  67.2 25.6 %shard_map.219 = (bf16[8,256,128]{2,1,0:T(8,128)(2,1)}, bf16[8,4,32,128]{3,2,1,0:T(8,128)(2,1)}) custom-call(bf16[8,256,128]{2,1,0:T(8,128)(2,1)} %bitcast.31, f32[8,4,32,128]{3,2,1,0:T(8,128)} %bitcast.32), custom_call_target="tpu_custom_call" | custom-call | tf_op jit(solution)/shard_map/pallas_call | solution.py:429
  92.8 4.1 %shard_map.220 = (f32[1024,128]{1,0:T(8,128)}, f32[256,128]{1,0:T(8,128)}, f32[128,128]{1,0:T(8,128)}, f32[256,128]{1,0:T(8,128)}, f32[128,128]{1,0:T(8,128)}, /*index=5*/f32[128,128]{1,0:T(8,128)}, f32[128,128]{1,0:T(8,128)}) custom-call(f32[1024,128]{1,0:T(8,128)} %get-tuple-element.39.d_owned_ref, bf16[2048,128]{1,0:T(8,128)(2,1)} %bitcast.33, ...), custom_call_target="tpu_custom_call" | custom-call | tf_op jit(solution)/shard_map/pallas_call | solution.py:429
  96.9 0.0 copy-done.2
  96.9 0.6 copy.38
  (1 shorter events, 0.0 us)
Async XLA Ops:
  7.3 14.5 %copy-start = (s32[1,4096]{1,0:T(1,128)S(1)}, s32[1,4096]{1,0:T(1,128)}, u32[]{:S(2)}) copy-start(s32[1,4096]{1,0:T(1,128)} %send_row_ref.1) | copy-start | bytes 49156
  8.4 15.4 %copy-start.1 = (s32[1,4096]{1,0:T(1,128)S(1)}, s32[1,4096]{1,0:T(1,128)}, u32[]{:S(2)}) copy-start(s32[1,4096]{1,0:T(1,128)} %param.19) | copy-start | bytes 49156
  67.2 29.7 %copy-start.2 = (bf16[128,128]{1,0:T(8,128)(2,1)S(1)}, bf16[128,128]{1,0:T(8,128)(2,1)}, u32[]{:S(2)}) copy-start(bf16[128,128]{1,0:T(8,128)(2,1)} %get-tuple-element.61) | copy-start | bytes 98308

commit v2 on v1

--- a/solution.py
+++ b/solution.py
@@ -11,9 +11,11 @@
 MESH = pl.DeviceIdType.MESH
 ACROSS = (-1, -1, -1, 0, 0, 1, 1, 1)
 ALONG = (-1, 0, 1, -1, 1, -1, 0, 1)
+SEND_ORDER = (0, 2, 5, 7, 3, 4, 1, 6)
 F32 = jnp.float32
 BF16 = jnp.bfloat16
 FOLDS = 4
+LANES = 128
 
 
 def mm(a, b):
@@ -32,9 +34,28 @@
     return 1.0 / (1.0 + jnp.exp(-v))
 
 
+def columns(row):
+    return jnp.concatenate(
+        [
+            jnp.transpose(jnp.broadcast_to(row[:, s : s + LANES], (LANES, LANES)))
+            for s in range(0, row.shape[1], LANES)
+        ],
+        axis=0,
+    )
+
+
+def alive(row, start, count):
+    ids = lax.broadcasted_iota(jnp.int32, row.shape, 1) + start
+    return jnp.where(ids < count, row, -1)
+
+
 def pick_lanes(col, width):
-    ids = lax.broadcasted_iota(jnp.int32, (col.shape[0], width), 1)
-    return jnp.where(ids == col, 1.0, 0.0).astype(BF16)
+    ids = lax.broadcasted_iota(jnp.int32, (col.shape[0], LANES), 1)
+    parts = [
+        jnp.where(ids == col - s, 1.0, 0.0).astype(BF16)[:, : min(LANES, width - s)]
+        for s in range(0, width, LANES)
+    ]
+    return jnp.concatenate(parts, axis=1)
 
 
 def pick_sublanes(row, start, height):
@@ -82,16 +103,8 @@
         table[:, j * latent : (j + 1) * latent] = rows(j * height, height)
 
 
-def outgoing_kernel(nodes_ref, col_ref, out_ref, table):
-    latent = nodes_ref.shape[1]
-    write_folded(table, lambda s, h: nodes_ref[s : s + h, :], latent)
-    step = 512 if col_ref.shape[0] % 512 == 0 else col_ref.shape[0]
-    for s in range(0, col_ref.shape[0], step):
-        out_ref[s : s + step, :] = gather_folded(col_ref[s : s + step, :], table[...]).astype(BF16)
-
-
 def forward_kernel(
-    chunk, nodes_ref, ghosts_ref, send_ref, recv_ref, recv_row_ref, pool_row_ref,
+    chunk, nodes_ref, ghosts_ref, send_ref, recv_ref, count_ref, pool_row_ref,
     wei_ref, weo_ref, wni_ref, wno_ref,
     fine_ref, window_ref, pre_ref, node_pre_ref, summed_ref,
     lookup, send_table, recv_table, wide,
@@ -104,20 +117,20 @@
 
     def edges(i, carry):
         at = pl.ds(pl.multiple_of(i * chunk, chunk), chunk)
-        recv = recv_ref[at, :]
-        pre = gather_folded(send_ref[at, :], send_table[...]) + gather_folded(recv, recv_table[...])
+        recv = columns(alive(recv_ref[:, at], i * chunk, count_ref[...]))
+        pre = gather_folded(columns(send_ref[:, at]), send_table[...]) + gather_folded(recv, recv_table[...])
         pre_ref[at, :] = pre
         act = (pre * sigmoid(pre)).astype(BF16)
         message = mm(act, weo_ref[...]).astype(BF16)
         wide[at, :] = spread_folds(message, fold_of(recv, rows // FOLDS))
         return carry
 
-    lax.fori_loop(0, send_ref.shape[0] // chunk, edges, 0)
+    lax.fori_loop(0, send_ref.shape[1] // chunk, edges, 0)
 
     def put(s, v):
         summed_ref[s : s + v.shape[0], :] = v.astype(BF16)
 
-    scatter_folded(recv_row_ref[...], wide, rows // FOLDS, min(256, rows // FOLDS), put)
+    scatter_folded(alive(recv_ref[...], 0, count_ref[...]), wide, rows // FOLDS, min(256, rows // FOLDS), put)
     node_pre = mm(nodes_ref[...], wni_ref[:latent, :]) + mm(summed_ref[...], wni_ref[latent:, :])
     node_pre_ref[...] = node_pre
     node_act = (node_pre * sigmoid(node_pre)).astype(BF16)
@@ -212,7 +225,7 @@
 
 
 def backward_kernel(
-    chunk, nodes_ref, ghosts_ref, recv_ref, recv_row_ref, send_ref, send_row_ref, pool_ref,
+    chunk, nodes_ref, ghosts_ref, recv_ref, count_ref, send_ref, pool_ref,
     wei_ref, weo_ref, wni_ref, wno_ref,
     pre_ref, node_pre_ref, summed_ref, reach_ref, d_fine_ref, g_ci_ref, g_co_ref,
     d_owned_ref, d_ghost_ref, g_ref,
@@ -222,7 +235,7 @@
     total_rows = rows + ghosts_ref.shape[0]
     nodes = nodes_ref[...]
     d_total = d_fine_ref[...].astype(F32) + 0.125 * mm(
-        pick_lanes(pool_ref[...], reach_ref.shape[0]), reach_ref[...]
+        pick_lanes(columns(pool_ref[...]), reach_ref.shape[0]), reach_ref[...]
     )
     d16 = d_total.astype(BF16)
     node_pre = node_pre_ref[...]
@@ -244,7 +257,7 @@
 
     def edges(i, carry):
         at = pl.ds(pl.multiple_of(i * chunk, chunk), chunk)
-        recv = recv_ref[at, :]
+        recv = columns(alive(recv_ref[:, at], i * chunk, count_ref[...]))
         d_message = gather_folded(recv, table[...]).astype(BF16)
         pre = pre_ref[at, :]
         sig = sigmoid(pre)
@@ -252,10 +265,10 @@
         g_out[...] += t_mm(act, d_message)
         d_pre = (mm_t(d_message, weo_ref[...]) * (sig * (1.0 + pre * (1.0 - sig)))).astype(BF16)
         recv_wide[at, :] = spread_folds(d_pre, fold_of(recv, height))
-        send_wide[at, :] = spread_folds(d_pre, fold_of(send_ref[at, :], total_rows // FOLDS))
+        send_wide[at, :] = spread_folds(d_pre, fold_of(columns(send_ref[:, at]), total_rows // FOLDS))
         return carry
 
-    lax.fori_loop(0, send_ref.shape[0] // chunk, edges, 0)
+    lax.fori_loop(0, send_ref.shape[1] // chunk, edges, 0)
     g_ref[base : base + latent, :] = g_out[...]
 
     def put_s(at, v):
@@ -264,8 +277,8 @@
     def put_r(at, v):
         sums_r[at : at + v.shape[0], :] = v.astype(BF16)
 
-    scatter_folded(recv_row_ref[...], recv_wide, height, min(256, height), put_r)
-    scatter_folded(send_row_ref[...], send_wide, total_rows // FOLDS, min(256, total_rows // FOLDS), put_s)
+    scatter_folded(alive(recv_ref[...], 0, count_ref[...]), recv_wide, height, min(256, height), put_r)
+    scatter_folded(send_ref[...], send_wide, total_rows // FOLDS, min(256, total_rows // FOLDS), put_s)
     w_send, w_recv = wei_ref[:latent, :], wei_ref[latent:, :]
     d_owned_ref[...] += mm_t(sums_s[:rows, :], w_send) + mm_t(sums_r[...], w_recv)
     d_ghost_ref[...] = mm_t(sums_s[rows:, :], w_send).astype(BF16)
@@ -333,13 +346,30 @@
             copies[k].wait_recv()
 
 
-def exchange_kernel(n_gx, n_gy, src_ref, dst_ref, send_sem, recv_sem):
+def ghost_row(rows_ref, count_ref, k):
+    return alive(rows_ref[0, k : k + 1, :], 0, count_ref[:, k : k + 1])
+
+
+def exchange_kernel(n_gx, n_gy, nodes_ref, rows_ref, count_ref, dst_ref, table, outgoing, send_sem, recv_sem):
     found = neighbours(n_gx, n_gy, 1)
     barrier = pltpu.get_barrier_semaphore()
     greet(barrier, found)
-    greeted(barrier, found)
-    copies = exchange_copies(found, src_ref, dst_ref, send_sem, recv_sem)
-    exchange_start(found, copies, dst_ref)
+    write_folded(table, lambda s, h: nodes_ref[s : s + h, :], nodes_ref.shape[1])
+    copies = exchange_copies(found, outgoing, dst_ref, send_sem, recv_sem)
+    for n, k in enumerate(SEND_ORDER):
+        outgoing[k] = gather_folded(columns(ghost_row(rows_ref, count_ref, k)), table[...]).astype(BF16)
+        if n == 0:
+            greeted(barrier, found)
+
+        @pl.when(found[k][1])
+        def _(k=k):
+            copies[k].start()
+
+    for k in range(len(found)):
+        @pl.when(jnp.logical_not(found[k][2]))
+        def _(k=k):
+            dst_ref[k] = jnp.zeros(dst_ref.shape[1:], dst_ref.dtype)
+
     exchange_wait(found, copies)
 
 
@@ -405,16 +435,20 @@
 
 
 def final_kernel(
-    scale, d_owned_ref, back_ref, col_ref, row_ref, total_ref,
+    scale, d_owned_ref, back_ref, rows_ref, count_ref, total_ref,
     nodes_out, ei_ref, eo_ref, ni_ref, no_ref, ci_ref, co_ref, wide,
 ):
     height = d_owned_ref.shape[0] // FOLDS
-    wide[...] = spread_folds(back_ref[...], fold_of(col_ref[...], height))
+    index = [ghost_row(rows_ref, count_ref, k) for k in range(rows_ref.shape[1])]
+    for k, row in enumerate(index):
+        wide[k * row.shape[1] : (k + 1) * row.shape[1], :] = spread_folds(
+            back_ref[k], fold_of(columns(row), height)
+        )
 
     def put(at, v):
         nodes_out[at : at + v.shape[0], :] = d_owned_ref[at : at + v.shape[0], :] + v
 
-    scatter_folded(row_ref[...], wide, height, min(256, height), put)
+    scatter_folded(jnp.concatenate(index, axis=1), wide, height, min(256, height), put)
     at = 0
     for ref in (ei_ref, eo_ref, ni_ref, no_ref, ci_ref, co_ref):
         ref[...] = total_ref[at : at + ref.shape[0], :].astype(F32) * scale
@@ -447,24 +481,14 @@
     co = d_coarse.shape[0]
     chunk = 512 if edges_n % 512 == 0 else edges_n
     dma = pltpu.SemaphoreType.DMA
-    live = jnp.arange(slots, dtype=jnp.int32)[None, :] < ghost_count[0][:, None]
-    ghost_index = jnp.where(live, ghost_rows[0], -1).reshape(1, ghosts_n)
-    ghost_col = ghost_index.reshape(ghosts_n, 1)
-    edge_live = jnp.arange(edges_n, dtype=jnp.int32) < edge_count[0]
-    recv_row = jnp.where(edge_live, edge_recv[0], -1).reshape(1, edges_n)
-    recv_col = recv_row.reshape(edges_n, 1)
-    send_row = edge_send
-    send_col = edge_send.reshape(edges_n, 1)
-    pool_col = pool_map.reshape(rows, 1)
+    edge_total = edge_count.reshape(1, 1)
     fold_rows = rows // FOLDS
     fold_all = (rows + ghosts_n) // FOLDS
 
-    (outgoing,) = call(
-        outgoing_kernel, [((ghosts_n, latent), BF16)],
-        [pltpu.VMEM((fold_rows, FOLDS * latent), BF16)], (nodes, ghost_col))
     (arrived,) = call(
         functools.partial(exchange_kernel, n_gx, n_gy), [((peers, slots, latent), BF16)],
-        [dma((peers,)), dma((peers,))], (outgoing.reshape(peers, slots, latent),), 0)
+        [pltpu.VMEM((fold_rows, FOLDS * latent), BF16), pltpu.VMEM((peers, slots, latent), BF16),
+         dma((peers,)), dma((peers,))], (nodes, ghost_rows, ghost_count), 0)
     ghosts = arrived.reshape(ghosts_n, latent)
     fine_out, window, pre, node_pre, summed = call(
         functools.partial(forward_kernel, chunk),
@@ -472,7 +496,7 @@
          ((rows, latent), F32), ((rows, latent), BF16)],
         [pltpu.VMEM((rows + ghosts_n, latent), BF16), pltpu.VMEM((fold_all, FOLDS * latent), BF16),
          pltpu.VMEM((fold_rows, FOLDS * latent), BF16), pltpu.VMEM((edges_n, FOLDS * latent), BF16)],
-        (nodes, ghosts, send_col, recv_col, recv_row, pool_map, w_edge_in, w_edge_out, w_node_in, w_node_out))
+        (nodes, ghosts, edge_send, edge_recv, edge_total, pool_map, w_edge_in, w_edge_out, w_node_in, w_node_out))
     coarse_out, reach, g_ci, g_co = call(
         functools.partial(coarse_kernel, n_gy),
         [((co, latent), BF16), ((co + 2 * BAND, latent), BF16), ((latent, latent), F32), ((latent, latent), F32)],
@@ -484,7 +508,7 @@
         [pltpu.VMEM((fold_rows, FOLDS * latent), BF16), pltpu.VMEM((edges_n, FOLDS * latent), BF16),
          pltpu.VMEM((edges_n, FOLDS * latent), BF16), pltpu.VMEM((rows + ghosts_n, latent), BF16),
          pltpu.VMEM((rows, latent), BF16), pltpu.VMEM((latent, latent), F32)],
-        (nodes, ghosts, recv_col, recv_row, send_col, send_row, pool_col, w_edge_in, w_edge_out, w_node_in,
+        (nodes, ghosts, edge_recv, edge_total, edge_send, pool_map, w_edge_in, w_edge_out, w_node_in,
          w_node_out, pre, node_pre, summed, reach, d_fine, g_ci, g_co))
     share = 8 * latent // (n_gx * n_gy)
     parts = (n_gx, n_gy, share, latent)
@@ -501,7 +525,7 @@
         [((rows, latent), F32), ((2 * latent, latent), F32), ((latent, latent), F32), ((2 * latent, latent), F32),
          ((latent, latent), F32), ((latent, latent), F32), ((latent, latent), F32)],
         [pltpu.VMEM((ghosts_n, FOLDS * latent), BF16)],
-        (d_owned, back.reshape(ghosts_n, latent), ghost_col, ghost_index, total.reshape(8 * latent, latent)))
+        (d_owned, back, ghost_rows, ghost_count, total.reshape(8 * latent, latent)))
     return (fine_out, coarse_out) + tuple(outs)
 
 

time: 97.9 us -> 78.4 us (0.80)
  Pallas kernels: 84.2 us -> 76.3 us
  local copies, waits for them, and re-layouts: 6.58 us -> 0.62 us
  other arithmetic: 5.3 us -> 0 us
    pallas_call x7 -> x6, Pallas kernels: 84.2 us -> 76.3 us  [call(): pl.pallas_call(kernel, out_shape=[jax.ShapeDtypeStruct(shape, kind) for s...]
    select_n x4 -> x0, other arithmetic: 4.57 us -> none  [the longest x2 2.86 us: body(): recv_row = jnp.where(edge_live, edge_recv[0], -1).reshape(1, edges_n)]
    reshape x2 -> x0, local copies, waits for them, and re-layouts: 3.75 us -> none  [the longest x1 2 us: body(): send_col = edge_send.reshape(edges_n, 1)]
    unnamed x11 -> x3, local copies, waits for them, and re-layouts: 2.19 us -> 0.62 us
where the time goes in v2:
time: 78.4 us; the launch traced here: 78.2 us
  Pallas kernels  76.3 us (97%)
  between operations  1.32 us (2%)
    pallas_call x6, Pallas kernels, call(): pl.pallas_call(kernel, out_shape=[jax.ShapeDtypeStruct(shape, kind) for s...  76.3 us

profile of v2, /device:TPU:0, one launch (start us, length us, event | category | flops | bytes accessed | tf_op | source)
XLA Modules:
  0.0 78.2 jit_solution(6402801092975972711)
XLA Ops:
  0.6 11.6 %shard_map.214 = bf16[8,256,128]{2,1,0:T(8,128)(2,1)} custom-call(bf16[1024,128]{1,0:T(8,128)(2,1)} %nodes_ref.5, s32[1,8,256]{2,1,0:T(8,128)} %rows_ref.3, s32[1,8]{1,0:T(1,128)} %count_ref.3), custom_call_target="tpu_custom_call" | custom-call | tf_op jit(solution)/shard_map/pallas_call | solution.py:463
  12.9 13.0 %shard_map.215 = (bf16[1024,128]{1,0:T(8,128)(2,1)}, f32[192,128]{1,0:T(8,128)}, f32[4096,128]{1,0:T(8,128)}, f32[1024,128]{1,0:T(8,128)}, bf16[1024,128]{1,0:T(8,128)(2,1)}) custom-call(bf16[1024,128]{1,0:T(8,128)(2,1)} %nodes_ref.5, bf16[2048,128]{1,0:T(8,128)(2,1)} %bitcast.7, s32[1,4096]{1,0:T(1,128)} %send_ref.3, s32[1,4096]{1,0:T(1,128)} %recv_ref.3, ...), custom_call_target="tpu_custom_call" | custom-call | tf_op jit(solution)/shard_map/pallas_call | solution.py:463
  25.9 9.3 %shard_map.216 = (bf16[128,128]{1,0:T(8,128)(2,1)}, bf16[192,128]{1,0:T(8,128)(2,1)}, f32[128,128]{1,0:T(8,128)}, f32[128,128]{1,0:T(8,128)}) custom-call(f32[192,128]{1,0:T(8,128)} %get-tuple-element.31.window_ref, bf16[128,128]{1,0:T(8,128)(2,1)} %d_coarse_ref.1, bf16[128,128]{1,0:T(8,128)(2,1)} %wci_ref.1, bf16[128,128]{1,0:T(8,128)(2,1)} %wco_ref.1), custom_call_target="tpu_custom_call" | custom-call | tf_op jit(solution)/shard_map/pallas_call | solution.py:463
  35.2 15.7 %shard_map.217 = (f32[1024,128]{1,0:T(8,128)}, bf16[2048,128]{1,0:T(8,128)(2,1)}, f32[1024,128]{1,0:T(8,128)}) custom-call(bf16[1024,128]{1,0:T(8,128)(2,1)} %nodes_ref.5, bf16[2048,128]{1,0:T(8,128)(2,1)} %bitcast.8, s32[1,4096]{1,0:T(1,128)} %recv_ref.3, s32[1,1]{1,0:T(1,128)} %bitcast.6.count_ref, s32[1,4096]{1,0:T(1,128)} %send_ref.3, ...), custom_call_target="tpu_custom_call" | custom-call | tf_op jit(solution)/shard_map/pallas_call | solution.py:463
  51.0 0.0 copy-start
  51.0 23.3 %shard_map.218 = (bf16[8,256,128]{2,1,0:T(8,128)(2,1)}, bf16[8,4,32,128]{3,2,1,0:T(8,128)(2,1)}) custom-call(bf16[8,256,128]{2,1,0:T(8,128)(2,1)} %bitcast.9, f32[8,4,32,128]{3,2,1,0:T(8,128)} %bitcast.10), custom_call_target="tpu_custom_call" | custom-call | tf_op jit(solution)/shard_map/pallas_call | solution.py:463
  74.3 3.3 %shard_map.219 = (f32[1024,128]{1,0:T(8,128)}, f32[256,128]{1,0:T(8,128)}, f32[128,128]{1,0:T(8,128)}, f32[256,128]{1,0:T(8,128)}, f32[128,128]{1,0:T(8,128)}, /*index=5*/f32[128,128]{1,0:T(8,128)}, f32[128,128]{1,0:T(8,128)}) custom-call(f32[1024,128]{1,0:T(8,128)} %get-tuple-element.39.d_owned_ref, bf16[8,256,128]{2,1,0:T(8,128)(2,1)} %get-tuple-element.42.back_ref, ...), custom_call_target="tpu_custom_call" | custom-call | tf_op jit(solution)/shard_map/pallas_call | solution.py:463
  77.6 0.0 copy-done
  77.6 0.6 copy.26
Async XLA Ops:
  51.0 26.6 %copy-start = (bf16[128,128]{1,0:T(8,128)(2,1)S(1)}, bf16[128,128]{1,0:T(8,128)(2,1)}, u32[]{:S(2)}) copy-start(bf16[128,128]{1,0:T(8,128)(2,1)} %get-tuple-element.61) | copy-start | bytes 98308
